TPU v7x, 128 devices: a whole 4x4x4 slice. The times are simulated.
128 devices in a mesh: row: 16 (over z_lo, x, core), col: 8 (over z_hi, y).
Axes of the slice: x: 4, y: 4, z: 4 (z_hi: 2, z_lo: 2; z = z_hi * 2 + z_lo), core: 2. Of those that a mesh axis runs over, the one named last changes fastest.
Arguments:
- density: bfloat16 [64, 5, 256, 256], P('row', None, 'col'), may hold values from -1 to 2, as said below
- pattern: int32 [64, 5], P('row'), may hold values from 0 to 1, as said below
- windows: int32 [256], P(('row', 'col')), may hold values from 0 to 125, as said below
- basis_values: bfloat16 [256, 4096, 384], P(('row', 'col')), may hold values from -6 to 6
- basis_grads: bfloat16 [3, 256, 4096, 384], P(None, ('row', 'col')), may hold values from -48 to 48
- weights: float32 [256, 4096], P(('row', 'col')), may hold values from 0.25 to 4
Outputs:
- purified: bfloat16 [64, 5, 256, 256], P('row', None, 'col')
- xc_matrix: float32 [64, 5, 256, 256], P('row', None, 'col')
- grid_density: float32 [256, 4096], P(('row', 'col'))
Inputs may be any that keep to these rules, and one draw needn't show every extreme that they name: density[i, d] is block (i, i + d - 2) of a symmetric matrix: density[i, d] equals density[i + d - 2, 4 - d] transposed; blocks whose column block lies outside the matrix are 0. pattern[i, d] = pattern[i + d - 2, 4 - d]; it is 1 for d = 1, 2, 3 where block i + d - 2 exists and 0 where it does not. Tile t lies on device t // 2 of the joined axes row+col; if that device has row index q, windows[t] lies between 2 * 4 q - 2 and 2 * 4 q + 2 * 4 - 1.
All inputs are finite; a program needn't handle non-finite values.
Results may differ from a plain program's by a relative error of at most 0.011.
Values may be sent and summed in bfloat16 or wider, within the bound.
A program may use at most 128 MiB of HBM per device.

v0:
```python
import jax
import jax.numpy as jnp
from jax import lax
from jax.sharding import Mesh
from jax.sharding import PartitionSpec as P

ITERS = 2
COL = ("col_0", "col_1")
ROW_COL = ("row", "col_0", "col_1")
slater_cx = 0.7386
kappa_pbe = 0.804
mu_pbe = 0.2195


def shifted_2(value, axis, by):
    length = lax.axis_size(axis)
    pairs = [(i, i + by) for i in range(length) if 0 <= i + by < length]
    return lax.ppermute(value, axis, pairs)


def padded(cells, sides, width):
    for axis, dim in sides:
        count = lax.axis_size(axis)
        ends = count - 1
        head = lax.slice_in_dim(cells, 0, width, axis=dim)
        tail = lax.slice_in_dim(cells, cells.shape[dim] - width, cells.shape[dim], axis=dim)
        cells = jnp.concatenate(
            [
                lax.ppermute(tail, axis, [(i, (i + 1) % count) for i in range(ends)]),
                cells,
                lax.ppermute(head, axis, [((i + 1) % count, i) for i in range(ends)]),
            ],
            axis=dim,
        )
    return cells


def in_order(pieces, dim):
    pieces = jnp.moveaxis(pieces, 0, dim)
    lengths = pieces.shape
    return pieces.reshape(*lengths[:dim], lengths[dim] * lengths[dim + 1], *lengths[dim + 2 :])


def sent_to_all(value, axis):
    length = lax.axis_size(axis)
    return lax.all_to_all(
        jnp.broadcast_to(value[None], (length, *value.shape)), axis, 0, 0, tiled=True
    )


def gather_directly(value, axis, dim):
    return in_order(sent_to_all(value, axis), dim)


def sum_in_order(pieces, axes, sequence):
    inside = pieces.shape[1:]
    pieces = pieces.reshape(*(lax.axis_size(a) for a in axes), *inside)
    pieces = jnp.moveaxis(pieces, sequence, range(len(axes))).reshape(-1, *inside)
    for k in sequence:
        pieces = lax.psum_scatter(pieces, axes[k], scatter_dimension=0, tiled=True)
    return pieces[0]


def cut_along(value, dim, length):
    before, after = (value.shape[:dim], value.shape[dim + 1 :])
    return jnp.moveaxis(value.reshape(*before, length, -1, *after), dim, 0)


def scatter_axes(value, axes, sequence, dim):
    length = lax.axis_size(axes)
    return sum_in_order(cut_along(value, dim, length), axes, sequence)


def energy_sum(point_density, grad_square):
    spread = jnp.sqrt(point_density * point_density + 1.0)
    reduced = grad_square / spread ** (8.0 / 3.0)
    enhance = 1.0 + kappa_pbe - kappa_pbe / (1.0 + mu_pbe * reduced / kappa_pbe)
    return jnp.sum(-slater_cx * spread ** (4.0 / 3.0) * enhance)


def tile_terms(values, grads, quadrature, window_block):
    functions = values.shape[1]
    points = values.shape[0]
    projected = jnp.dot(values, window_block, preferred_element_type=jnp.float32)
    point_density = jnp.sum(projected * values.astype(jnp.float32), axis=1) / functions
    slopes = 2.0 * jnp.sum(projected[None] * grads.astype(jnp.float32), axis=2) / functions
    grad_square = jnp.sum(slopes * slopes, axis=0)
    by_density, by_gradient = jax.grad(energy_sum, argnums=(0, 1))(point_density, grad_square)
    scaled = quadrature / points
    weighted = (0.5 * by_density * scaled)[:, None] * values.astype(jnp.float32)
    weighted = weighted + jnp.sum(
        ((2.0 * by_gradient * scaled)[None] * slopes)[:, :, None] * grads.astype(jnp.float32),
        axis=0,
    )
    weighted = weighted.astype(jnp.bfloat16)
    one_side = lax.dot_general(
        values, weighted, (((0,), (0,)), ((), ())), preferred_element_type=jnp.float32
    )
    return (point_density, one_side + one_side.T)


def band_product(left, right_padded):
    blocks = left.shape[0]
    total = None
    for offset_step in range(5):
        shifted = right_padded[offset_step : offset_step + blocks]
        widened = jnp.pad(shifted, ((0, 0), (2, 2), (0, 0), (0, 0)))
        picked = widened[:, 4 - offset_step : 9 - offset_step]
        term = jnp.einsum(
            "brk,bdkc->bdrc", left[:, offset_step], picked, preferred_element_type=jnp.float32
        )
        total = term if total is None else total + term
    return total


def window_of(band_three, lead, offset, functions):
    paired = lax.dynamic_slice_in_dim(band_three, lead, 2, 0)
    upper = jnp.concatenate([paired[0, 1], paired[0, 2]], axis=1)
    lower = jnp.concatenate([paired[1, 0], paired[1, 1]], axis=1)
    dense = jnp.concatenate([upper, lower], axis=0)
    return lax.dynamic_slice(dense, (offset, offset), (functions, functions))


def spread_term(summed, term, lead, offset):
    width = summed.shape[2]
    dense = lax.dynamic_update_slice(
        jnp.zeros((2 * width, 2 * width), summed.dtype), term, (offset, offset)
    )
    nothing = jnp.zeros((width, width), summed.dtype)
    upper = jnp.stack([nothing, dense[:width, :width], dense[:width, width:]])
    lower = jnp.stack([dense[width:, :width], dense[width:, width:], nothing])
    increment = jnp.stack([upper, lower])
    paired = lax.dynamic_slice_in_dim(summed, lead, 2, 0)
    return lax.dynamic_update_slice_in_dim(summed, paired + increment, lead, 0)


def edge_rows(summed):
    blocks = summed.shape[0] - 2
    from_above = shifted_2(summed[0].astype(jnp.bfloat16), "row", -1).astype(jnp.float32)
    from_below = shifted_2(summed[blocks + 1].astype(jnp.bfloat16), "row", 1).astype(jnp.float32)
    own_rows = summed[1 : blocks + 1]
    return jnp.concatenate(
        [
            own_rows[:1] + from_below[None],
            own_rows[1 : blocks - 1],
            own_rows[blocks - 1 :] + from_above[None],
        ],
        axis=0,
    )


def on_device(density, pattern, windows, basis_values, basis_grads, weights):
    row_index = lax.axis_index("row")
    band_rows = density.shape[0]
    functions = basis_values.shape[2]
    step_size = functions // 3
    kept = (pattern > 0)[:, :, None, None]
    current = jnp.where(kept, density, jnp.zeros_like(density))
    for iteration in range(ITERS):
        near_right = padded(current, (("row", 0),), 2)
        right_full = lax.all_gather(near_right, COL, axis=2, tiled=True)
        square = jnp.where(kept, band_product(current, right_full), 0.0).astype(jnp.bfloat16)
        cubic = band_product(square, right_full)
        current = jnp.where(kept, 3.0 * square.astype(jnp.float32) - 2.0 * cubic, 0.0).astype(
            jnp.bfloat16
        )
    rows_band = gather_directly(current[:, 1:4], COL, 2)
    near = padded(rows_band, (("row", 0),), 1)
    tiles_here = windows.shape[0]
    points = basis_values.shape[1]
    block_size = near.shape[2]

    def one_tile(tile_index, carry):
        summed, densities = carry
        position = tile_index.astype(jnp.int32)
        start_step = windows[position]
        lead = start_step // 2 - (band_rows * row_index - 1)
        offset = start_step % 2 * step_size
        window_block = window_of(near, lead, offset, functions)
        values = lax.dynamic_index_in_dim(basis_values, position, 0, keepdims=False)
        grads = lax.dynamic_index_in_dim(basis_grads, position, 1, keepdims=False)
        quadrature = lax.dynamic_index_in_dim(weights, position, 0, keepdims=False)
        point_density, contribution = tile_terms(values, grads, quadrature, window_block)
        summed = spread_term(summed, contribution, lead, offset)
        densities = lax.dynamic_update_index_in_dim(densities, point_density, position, 0)
        return (summed, densities)

    start_carry = (
        jnp.zeros((band_rows + 2, 3, block_size, block_size), jnp.float32),
        jnp.zeros((tiles_here, points), jnp.float32),
    )
    local_terms, densities = lax.fori_loop(0, tiles_here, one_tile, start_carry)
    owner_part = scatter_axes(local_terms.astype(jnp.bfloat16), COL, (1, 0), 2).astype(jnp.float32)
    mine = edge_rows(owner_part)
    xc_matrix = jnp.where(kept, jnp.pad(mine, ((0, 0), (1, 1), (0, 0), (0, 0))), 0.0)
    return (current, xc_matrix, densities)


def solution(mesh):
    torus = Mesh(mesh.devices.reshape(mesh.shape["row"], 2, 4), ("row", "col_0", "col_1"))
    placed = (
        P("row", None, COL, None),
        P("row", None),
        P(ROW_COL),
        P(ROW_COL, None, None),
        P(None, ROW_COL, None, None),
        P(ROW_COL, None),
    )
    return jax.shard_map(
        on_device,
        mesh=torus,
        in_specs=placed,
        out_specs=(P("row", None, COL, None), P("row", None, COL, None), P(ROW_COL, None)),
        check_vma=False,
    )
```

profile of v0, /device:TPU:7, one launch (start us, length us, event | category | flops | bytes accessed | tf_op | source)
XLA Modules:
  0.0 434.2 jit_solution(14375397627598703558)
XLA Ops:
  7.2 0.7 broadcast_compare_fusion
  8.0 1.1 copy_select_fusion
  9.1 4.0 collective-permute-start
  13.1 1.9 collective-permute-start.1
  15.4 6.5 %collective-permute-done.1 = bf16[2,5,32,256]{3,2,0,1:T(8,128)(2,1)S(1)} collective-permute-done((bf16[2,5,32,256]{3,2,0,1:T(8,128)(2,1)S(1)}, bf16[2,5,32,256]{3,2,0,1:T(8,128)(2,1)S(1)}, u32[]{:S(2)}, u32[]{:S(2)}) %collective-permute-start.1) | collective-permute-done | bytes 163872 | tf_op jit(solution)/shard_map/ppermute | solution.py:31
  21.9 0.9 pad_maximum_fusion.1
  22.9 80.5 %all-gather.3.cloned.1.call-done = bf16[8,5,256,256]{3,2,0,1:T(8,128)(2,1)} async-done(((bf16[8,5,32,256]{3,2,0,1:T(8,128)(2,1)}), bf16[8,5,256,256]{3,2,0,1:T(8,128)(2,1)}) %all-gather.3.cloned.1.call-update) | async-done | bytes 5242896 | tf_op jit(solution)/shard_map/all_gather | solution.py:161
  103.4 4.5 %fusion.153 = (bf16[4,5,256,256]{3,2,0,1:T(8,128)(2,1)S(1)}, bf16[4,5,256,256]{3,2,0,1:T(8,128)(2,1)S(1)}, bf16[4,5,256,256]{3,2,0,1:T(8,128)(2,1)S(1)}, bf16[4,5,256,256]{3,2,0,1:T(8,128)(2,1)S(1)}) fusion(bf16[8,5,256,256]{3,2,0,1:T(8,128)(2,1)} %all-gather.3.cloned.1.call-done), kind=kLoop, calls=%fused_computation.165 | loop fusion | bytes 20971520 | tf_op jit(solution)/shard_map/slice | solution.py:106
  109.7 1.7 copy-done.1
  111.3 0.5 fusion.128
  113.6 0.6 fusion.113
  114.2 3.6 collective-permute-start.2
  117.8 1.9 collective-permute-start.3
  120.0 6.5 %collective-permute-done.3 = bf16[2,5,32,256]{3,2,0,1:T(8,128)(2,1)S(1)} collective-permute-done((bf16[2,5,32,256]{3,2,0,1:T(8,128)(2,1)S(1)}, bf16[2,5,32,256]{3,2,0,1:T(8,128)(2,1)S(1)}, u32[]{:S(2)}, u32[]{:S(2)}) %collective-permute-start.3) | collective-permute-done | bytes 163872 | tf_op jit(solution)/shard_map/ppermute | solution.py:31
  126.5 0.9 pad_maximum_fusion.2
  127.5 77.1 %all-gather.5.cloned.1.call-done = bf16[8,5,256,256]{3,2,0,1:T(8,128)(2,1)} async-done(((bf16[8,5,32,256]{3,2,0,1:T(8,128)(2,1)}), bf16[8,5,256,256]{3,2,0,1:T(8,128)(2,1)}) %all-gather.5.cloned.1.call-update) | async-done | bytes 5242896 | tf_op jit(solution)/shard_map/all_gather | solution.py:161
  204.6 4.5 %fusion.152 = (bf16[4,5,256,256]{3,2,0,1:T(8,128)(2,1)S(1)}, bf16[4,5,256,256]{3,2,0,1:T(8,128)(2,1)S(1)}, bf16[4,5,256,256]{3,2,0,1:T(8,128)(2,1)S(1)}, bf16[4,5,256,256]{3,2,0,1:T(8,128)(2,1)S(1)}) fusion(bf16[8,5,256,256]{3,2,0,1:T(8,128)(2,1)} %all-gather.5.cloned.1.call-done), kind=kLoop, calls=%fused_computation.164 | loop fusion | bytes 20971520 | tf_op jit(solution)/shard_map/slice | solution.py:106
  210.9 1.7 copy-done.2
  212.5 0.5 fusion.125
  213.5 0.5 fusion.40
  214.8 0.6 fusion.119
  215.6 24.1 %all_to_all.5 = bf16[8,4,3,32,256]{4,3,2,1,0:T(8,128)(2,1)S(1)} all-to-all(bf16[8,4,3,32,256]{4,3,2,1,0:T(8,128)(2,1)S(1)} %broadcast_in_dim.83), channel_id=1, replica_groups=mesh['row'=16,'col_0'=2,'col_1'=4] {'col_0','col_1'}, dimensions={0} | all-to-all | bytes 3145728 | tf_op jit(solution)/shard_map/all_to_all | solution.py:46
  240.0 4.8 %collective-permute-start.4 = (bf16[1,3,256,256]{3,2,1,0:T(8,128)(2,1)S(1)}, bf16[1,3,256,256]{3,2,1,0:T(8,128)(2,1)S(1)}, u32[]{:S(2)}, u32[]{:S(2)}) collective-permute-start(bf16[1,3,256,256]{3,2,1,0:T(8,128)(2,1)S(1)} %bitcast.239), channel_id=1, source_target_pairs={{0,8},{8,16},{16,24},{24,32},{32,40},{40,48},{48,56},{56,64},{64,7... | collective-permute-start | bytes 1179656 | tf_op jit(solution)/shard_map/ppermute | solution.py:29
  244.8 2.1 collective-permute-start.5
  246.9 2.6 collective-permute-done.4
  249.5 6.5 %collective-permute-done.5 = bf16[1,3,256,256]{3,2,1,0:T(8,128)(2,1)S(1)} collective-permute-done((bf16[1,3,256,256]{3,2,1,0:T(8,128)(2,1)S(1)}, bf16[1,3,256,256]{3,2,1,0:T(8,128)(2,1)S(1)}, u32[]{:S(2)}, u32[]{:S(2)}) %collective-permute-start.5) | collective-permute-done | bytes 393248 | tf_op jit(solution)/shard_map/ppermute | solution.py:31
  256.0 1.7 pad_maximum_fusion
  257.7 2.6 broadcast_in_dim.81
  260.3 99.6 %while.18 = (s32[]{:T(128)}, f32[6,3,256,256]{3,2,1,0:T(8,128)}, f32[2,4096]{1,0:T(2,128)}, s32[2]{0:T(128)}, s32[]{:T(128)}, /*index=5*/bf16[2,4096,384]{2,1,0:...) while((s32[]{:T(128)}, f32[6,3,256,256]{3,2,1,0:T(8,128)}, ...), condition=%wide.region_5.6_spmd, body=%wide.region_0.5_spmd.sunk | while | flops 2456809472 | bytes 116916952 | solution.py:192
  260.3 1.3 dynamic_slice.135
  264.2 0.7 dynamic-slice_bitcast_fusion.5
  264.9 2.2 constant_dynamic-slice_fusion.2
  267.1 3.0 copy.330
  270.1 7.4 %multiply_reduce_fusion.4 = (f32[4096]{0:T(1024)S(1)}, f32[4096,384]{0,1:T(8,128)}) fusion(bf16[1,4096,384]{1,2,0:T(8,128)(2,1)} %copy.330, s32[]{:T(128)S(6)} %select_n.130, bf16[256,256]{1,0:T(8,128)(2,1)} %get-tuple-element.462, bf16[256,256]{1,0:T(8,128)(2,1)S(1)} %get-tuple-element.463, bf16[256,256]{1,0:T(8,128)(2,1)S(1)} %get-tuple-element.464, ...), kind=kOutput, calls=%fused_computation.6.clone.1 | convolution fusion | flops 1213853696 | bytes 13123588 | tf_op jit(solution)/shard_map/while/body/eval_jaxpr/dot_general | solution.py:84
  277.5 6.6 %copy.331 = f32[4096,384]{1,0:T(8,128)} copy(f32[4096,384]{0,1:T(8,128)} %get-tuple-element.466) | data formatting | bytes 12582912 | tf_op jit(solution)/shard_map/while/body/eval_jaxpr/dot_general | solution.py:84
  284.1 6.8 %fusion.169 = f32[3,4096]{1,0:T(4,128)S(1)} fusion(f32[4096,384]{1,0:T(8,128)} %copy.331, bf16[3,2,4096,384]{3,2,1,0:T(8,128)(2,1)} %get-tuple-element.521, s32[]{:T(128)} %get-tuple-element.495), kind=kLoop, calls=%fused_computation.2.clone.1 | loop fusion | flops 14143488 | bytes 15777796 | tf_op jit(solution)/shard_map/while/body/eval_jaxpr/reduce_sum | solution.py:86
  291.4 9.9 %fusion.170 = f32[4096,384]{1,0:T(8,128)S(1)} fusion(f32[3,4096]{1,0:T(4,128)S(1)} %broadcast_multiply_fusion.5, bf16[3,2,4096,384]{3,2,1,0:T(8,128)(2,1)} %get-tuple-element.521, s32[]{:T(128)} %get-tuple-element.495), kind=kLoop, calls=%fused_computation.3.clone.1 | loop fusion | flops 12582912 | bytes 15777796 | tf_op jit(solution)/shard_map/while/body/eval_jaxpr/reduce_sum | solution.py:91
  301.3 3.2 fusion.172
  304.5 1.4 copy.332
  306.4 2.9 fusion.174
  309.5 0.6 copy-done.12
  310.1 1.3 dynamic_slice.135
  314.0 0.7 dynamic-slice_bitcast_fusion.5
  314.7 2.2 constant_dynamic-slice_fusion.2
  316.9 3.0 copy.330
  319.9 7.3 %multiply_reduce_fusion.4 = (f32[4096]{0:T(1024)S(1)}, f32[4096,384]{0,1:T(8,128)}) fusion(bf16[1,4096,384]{1,2,0:T(8,128)(2,1)} %copy.330, s32[]{:T(128)S(6)} %select_n.130, bf16[256,256]{1,0:T(8,128)(2,1)} %get-tuple-element.462, bf16[256,256]{1,0:T(8,128)(2,1)S(1)} %get-tuple-element.463, bf16[256,256]{1,0:T(8,128)(2,1)S(1)} %get-tuple-element.464, ...), kind=kOutput, calls=%fused_computation.6.clone.1 | convolution fusion | flops 1213853696 | bytes 13123588 | tf_op jit(solution)/shard_map/while/body/eval_jaxpr/dot_general | solution.py:84
  327.2 6.6 %copy.331 = f32[4096,384]{1,0:T(8,128)} copy(f32[4096,384]{0,1:T(8,128)} %get-tuple-element.466) | data formatting | bytes 12582912 | tf_op jit(solution)/shard_map/while/body/eval_jaxpr/dot_general | solution.py:84
  333.8 6.8 %fusion.169 = f32[3,4096]{1,0:T(4,128)S(1)} fusion(f32[4096,384]{1,0:T(8,128)} %copy.331, bf16[3,2,4096,384]{3,2,1,0:T(8,128)(2,1)} %get-tuple-element.521, s32[]{:T(128)} %get-tuple-element.495), kind=kLoop, calls=%fused_computation.2.clone.1 | loop fusion | flops 14143488 | bytes 15777796 | tf_op jit(solution)/shard_map/while/body/eval_jaxpr/reduce_sum | solution.py:86
  341.1 9.9 %fusion.170 = f32[4096,384]{1,0:T(8,128)S(1)} fusion(f32[3,4096]{1,0:T(4,128)S(1)} %broadcast_multiply_fusion.5, bf16[3,2,4096,384]{3,2,1,0:T(8,128)(2,1)} %get-tuple-element.521, s32[]{:T(128)} %get-tuple-element.495), kind=kLoop, calls=%fused_computation.3.clone.1 | loop fusion | flops 12582912 | bytes 15777796 | tf_op jit(solution)/shard_map/while/body/eval_jaxpr/reduce_sum | solution.py:91
  351.1 3.2 fusion.172
  354.3 1.4 copy.332
  356.1 3.0 fusion.174
  359.3 0.6 copy-done.12
  359.9 2.6 convert_element_type.116
  362.5 1.7 copy.273
  364.3 28.8 %reduce-scatter.3.cloned.1.call-done = bf16[2,6,3,32,256]{4,3,2,1,0:T(8,128)(2,1)} async-done(((bf16[8,6,3,32,256]{4,3,2,1,0:T(8,128)(2,1)}), bf16[2,6,3,32,256]{4,3,2,1,0:T(8,128)(2,1)}) %reduce-scatter.3.cloned.1.call-update) | async-done | bytes 589840 | tf_op jit(solution)/shard_map/reduce_scatter | solution.py:60
  393.2 21.4 %reduce-scatter.5.cloned.1.call-done = bf16[1,6,3,32,256]{4,3,2,1,0:T(8,128)(2,1)} async-done(((bf16[2,6,3,32,256]{4,3,2,1,0:T(8,128)(2,1)}), bf16[1,6,3,32,256]{4,3,2,1,0:T(8,128)(2,1)}) %reduce-scatter.5.cloned.1.call-update) | async-done | bytes 294928 | tf_op jit(solution)/shard_map/reduce_scatter | solution.py:60
  414.5 0.8 slice_bitcast_fusion.48
  415.4 3.0 collective-permute-start.6
  418.4 0.7 copy.277
  419.1 1.9 collective-permute-start.7
  421.0 1.0 convert_element_type.117
  422.1 4.5 %collective-permute-done.7 = bf16[3,32,256]{2,1,0:T(8,128)(2,1)S(1)} collective-permute-done((bf16[3,32,256]{2,1,0:T(8,128)(2,1)S(1)}, bf16[3,32,256]{2,1,0:T(8,128)(2,1)S(1)}, u32[]{:S(2)}, u32[]{:S(2)}) %collective-permute-start.7) | collective-permute-done | bytes 49184 | tf_op jit(solution)/shard_map/ppermute | solution.py:18
  426.8 0.9 copy.278
  (94 shorter events, 10.2 us)
Async XLA Ops:
  7.2 96.2 %all-gather.3.cloned.1.call-start = ((), (), s32[]{:S(2)}) async-start(), calls=%async_computation.3 | async-start | bytes 5898240 | tf_op jit(solution)/shard_map/all_gather | solution.py:161
  8.0 206.8 %copy-start.9 = (pred[4,5]{0,1:T(8,128)(4,1)}, pred[4,5]{0,1:T(8,128)(4,1)S(1)}, u32[]{:S(2)}) copy-start(pred[4,5]{0,1:T(8,128)(4,1)S(1)} %copy.226) | copy-start | bytes 64
  9.1 6.3 %collective-permute-start = (bf16[2,5,32,256]{3,2,0,1:T(8,128)(2,1)S(1)}, bf16[2,5,32,256]{3,2,0,1:T(8,128)(2,1)S(1)}, u32[]{:S(2)}, u32[]{:S(2)}) collective-permute-start(bf16[2,5,32,256]{3,2,0,1:T(8,128)(2,1)S(1)} %get-tuple-element.389), channel_id=1, source_target_pairs={{0,8},{8,16},{16,24},{24,32},{32,40},{40,48},{48,56},{56,64},{64,7... | collective-permute-start | bytes 491528 | tf_op jit(solution)/shard_map/ppermute | solution.py:29
  13.1 8.7 %collective-permute-start.1 = (bf16[2,5,32,256]{3,2,0,1:T(8,128)(2,1)S(1)}, bf16[2,5,32,256]{3,2,0,1:T(8,128)(2,1)S(1)}, u32[]{:S(2)}, u32[]{:S(2)}) collective-permute-start(bf16[2,5,32,256]{3,2,0,1:T(8,128)(2,1)S(1)} %get-tuple-element.390), channel_id=1, source_target_pairs={{8,0},{16,8},{24,16},{32,24},{40,32},{48,40},{56,48},{64,56},{72,6... | collective-permute-start | bytes 491528 | tf_op jit(solution)/shard_map/ppermute | solution.py:31
  22.8 181.8 %all-gather.5.cloned.1.call-start = ((), (), s32[]{:S(2)}) async-start(), calls=%async_computation.4 | async-start | bytes 5898240 | tf_op jit(solution)/shard_map/all_gather | solution.py:161
  108.8 2.5 copy-start.1
  114.2 5.8 %collective-permute-start.2 = (bf16[2,5,32,256]{3,2,0,1:T(8,128)(2,1)S(1)}, bf16[2,5,32,256]{3,2,0,1:T(8,128)(2,1)S(1)}, u32[]{:S(2)}, u32[]{:S(2)}) collective-permute-start(bf16[2,5,32,256]{3,2,0,1:T(8,128)(2,1)S(1)} %get-tuple-element.387), channel_id=1, source_target_pairs={{0,8},{8,16},{16,24},{24,32},{32,40},{40,48},{48,56},{56,64},{64,7... | collective-permute-start | bytes 491528 | tf_op jit(solution)/shard_map/ppermute | solution.py:29
  117.8 8.7 %collective-permute-start.3 = (bf16[2,5,32,256]{3,2,0,1:T(8,128)(2,1)S(1)}, bf16[2,5,32,256]{3,2,0,1:T(8,128)(2,1)S(1)}, u32[]{:S(2)}, u32[]{:S(2)}) collective-permute-start(bf16[2,5,32,256]{3,2,0,1:T(8,128)(2,1)S(1)} %get-tuple-element.388), channel_id=1, source_target_pairs={{8,0},{16,8},{24,16},{32,24},{40,32},{48,40},{56,48},{64,56},{72,6... | collective-permute-start | bytes 491528 | tf_op jit(solution)/shard_map/ppermute | solution.py:31
  127.5 265.7 %reduce-scatter.3.cloned.1.call-start = ((), (), s32[]{:S(2)}) async-start(), calls=%async_computation.5 | async-start | bytes 2949120 | tf_op jit(solution)/shard_map/reduce_scatter | solution.py:60
  210.0 2.5 copy-start.2
  215.4 24.4 %copy-start.6 = (bf16[4,5,32,256]{3,2,0,1:T(8,128)(2,1)}, bf16[4,5,32,256]{3,2,0,1:T(8,128)(2,1)S(1)}, u32[]{:S(2)}) copy-start(bf16[4,5,32,256]{3,2,0,1:T(8,128)(2,1)S(1)} %fusion.119) | copy-start | bytes 983044
  239.9 16.1 %copy-start.5 = (bf16[8,4,3,32,256]{4,3,0,2,1:T(8,128)(2,1)}, bf16[8,4,3,32,256]{4,3,0,2,1:T(8,128)(2,1)S(1)}, u32[]{:S(2)}) copy-start(bf16[8,4,3,32,256]{4,3,0,2,1:T(8,128)(2,1)S(1)} %copy.326) | copy-start | bytes 4718596
  240.0 9.5 %collective-permute-start.4 = (bf16[1,3,256,256]{3,2,1,0:T(8,128)(2,1)S(1)}, bf16[1,3,256,256]{3,2,1,0:T(8,128)(2,1)S(1)}, u32[]{:S(2)}, u32[]{:S(2)}) collective-permute-start(bf16[1,3,256,256]{3,2,1,0:T(8,128)(2,1)S(1)} %bitcast.239), channel_id=1, source_target_pairs={{0,8},{8,16},{16,24},{24,32},{32,40},{40,48},{48,56},{56,64},{64,7... | collective-permute-start | bytes 1179656 | tf_op jit(solution)/shard_map/ppermute | solution.py:29
  244.8 11.2 %collective-permute-start.5 = (bf16[1,3,256,256]{3,2,1,0:T(8,128)(2,1)S(1)}, bf16[1,3,256,256]{3,2,1,0:T(8,128)(2,1)S(1)}, u32[]{:S(2)}, u32[]{:S(2)}) collective-permute-start(bf16[1,3,256,256]{3,2,1,0:T(8,128)(2,1)S(1)} %bitcast.238), channel_id=1, source_target_pairs={{8,0},{16,8},{24,16},{32,24},{40,32},{48,40},{56,48},{64,56},{72,6... | collective-permute-start | bytes 1179656 | tf_op jit(solution)/shard_map/ppermute | solution.py:31
  260.3 4.6 %copy-start.3 = (bf16[6,3,256,256]{3,2,1,0:T(8,128)(2,1)}, bf16[6,3,256,256]{3,2,1,0:T(8,128)(2,1)S(1)}, u32[]{:S(2)}) copy-start(bf16[6,3,256,256]{3,2,1,0:T(8,128)(2,1)S(1)} %get-tuple-element.520) | copy-start | bytes 7077892 | tf_op jit(solution)/shard_map/while
  284.1 6.9 %copy-start.8 = (f32[2,4096]{1,0:T(2,128)S(1)}, f32[2,4096]{1,0:T(2,128)}, u32[]{:S(2)}) copy-start(f32[2,4096]{1,0:T(2,128)} %get-tuple-element.522) | copy-start | bytes 98308 | tf_op jit(solution)/shard_map/while
  304.5 1.5 copy-start
  306.4 2.9 copy-start.11
  306.4 3.7 copy-start.4
  309.5 0.6 copy-start.12
  310.1 4.6 %copy-start.3 = (bf16[6,3,256,256]{3,2,1,0:T(8,128)(2,1)}, bf16[6,3,256,256]{3,2,1,0:T(8,128)(2,1)S(1)}, u32[]{:S(2)}) copy-start(bf16[6,3,256,256]{3,2,1,0:T(8,128)(2,1)S(1)} %get-tuple-element.520) | copy-start | bytes 7077892 | tf_op jit(solution)/shard_map/while
  333.8 6.9 %copy-start.8 = (f32[2,4096]{1,0:T(2,128)S(1)}, f32[2,4096]{1,0:T(2,128)}, u32[]{:S(2)}) copy-start(f32[2,4096]{1,0:T(2,128)} %get-tuple-element.522) | copy-start | bytes 98308 | tf_op jit(solution)/shard_map/while
  354.3 1.5 copy-start
  356.1 3.0 copy-start.11
  356.1 3.7 copy-start.4
  359.2 0.6 copy-start.12
  364.2 54.1 %copy-start.7 = (bf16[4,5,32,256]{3,2,0,1:T(8,128)(2,1)S(1)}, bf16[4,5,32,256]{3,2,0,1:T(8,128)(2,1)}, u32[]{:S(2)}) copy-start(bf16[4,5,32,256]{3,2,0,1:T(8,128)(2,1)} %copy-done.6) | copy-start | bytes 983044
  364.3 62.4 %copy-start.10 = (pred[4,5]{0,1:T(8,128)(4,1)S(1)}, pred[4,5]{0,1:T(8,128)(4,1)}, u32[]{:S(2)}) copy-start(pred[4,5]{0,1:T(8,128)(4,1)} %copy-done.9) | copy-start | bytes 64
  364.3 50.3 %reduce-scatter.5.cloned.1.call-start = ((), (), s32[]{:S(2)}) async-start(), calls=%async_computation.6 | async-start | bytes 884736 | tf_op jit(solution)/shard_map/reduce_scatter | solution.py:60
  415.4 6.7 %collective-permute-start.6 = (bf16[3,32,256]{2,1,0:T(8,128)(2,1)S(1)}, bf16[3,32,256]{2,1,0:T(8,128)(2,1)S(1)}, u32[]{:S(2)}, u32[]{:S(2)}) collective-permute-start(bf16[3,32,256]{2,1,0:T(8,128)(2,1)S(1)} %get-tuple-element.391), channel_id=1, source_target_pairs={{0,8},{8,16},{16,24},{24,32},{32,40},{40,48},{48,56},{56,64},{64,7... | collective-permute-start | bytes 147464 | tf_op jit(solution)/shard_map/ppermute | solution.py:18
  419.1 7.5 %collective-permute-start.7 = (bf16[3,32,256]{2,1,0:T(8,128)(2,1)S(1)}, bf16[3,32,256]{2,1,0:T(8,128)(2,1)S(1)}, u32[]{:S(2)}, u32[]{:S(2)}) collective-permute-start(bf16[3,32,256]{2,1,0:T(8,128)(2,1)S(1)} %get-tuple-element.392), channel_id=1, source_target_pairs={{8,0},{16,8},{24,16},{32,24},{40,32},{48,40},{56,48},{64,56},{72,6... | collective-permute-start | bytes 147464 | tf_op jit(solution)/shard_map/ppermute | solution.py:18
Sparse Core Ops, SparseCore 0:
  22.9 80.3 all-gather.2
  127.6 76.9 all-gather.4
  364.4 28.7 reduce-scatter.2
  395.4 19.1 reduce-scatter.4
where the time goes:
time: 435 us; the launch traced here: 434 us
  waiting for transfers between devices  235 us (54%)
  local copies, waits for them, and re-layouts  52 us (12%)
  other arithmetic  49.7 us (11%)
  matrix products  30.2 us (7%)
  blocking collectives  24.1 us (6%)
  starting transfers between devices  23.4 us (5%)
  between operations  14.1 us (3%)
  loops' own time  5.52 us (1%)
    all_gather x2, waiting for transfers between devices, on_device(): right_full = lax.all_gather(near_right, COL, axis=2, tiled=True)  158 us
    reduce_scatter x2, waiting for transfers between devices, sum_in_order(): pieces = lax.psum_scatter(pieces, axes[k], scatter_dimension=0, tiled=True)  50.2 us
    all_to_all x1, blocking collectives, sent_to_all(): lax.all_to_all(jnp.broadcast_to(value[None], (length, *value.shape)), axi...  24.1 us
    reduce_sum x2, other arithmetic, tile_terms(): jnp.sum(((2.0 * by_gradient * scaled)[None] * slopes)[:, :, None] * grads...  19.9 us
    ppermute x3, waiting for transfers between devices, padded(): lax.ppermute(head, axis, [((i + 1) % count, i) for i in range(ends)])  19.5 us
    dot_general x2, matrix products, tile_terms(): jnp.dot(values, window_block, preferred_element_type=jnp.float32)  14.7 us
    reduce_sum x2, other arithmetic, tile_terms(): jnp.sum(projected[None] * grads.astype(jnp.float32), axis=2)  13.6 us
    dot_general x2, local copies, waits for them, and re-layouts, tile_terms(): jnp.dot(values, window_block, preferred_element_type=jnp.float32)  13.1 us
  transfers between devices with their start and end apart: 12, of which 11 were waited for; matrix products, arithmetic and copies ran while one was open for 0% of the time, Pallas kernels for 0%

commit v1 on v0

--- a/solution.py
+++ b/solution.py
@@ -158,7 +158,9 @@
     current = jnp.where(kept, density, jnp.zeros_like(density))
     for iteration in range(ITERS):
         near_right = padded(current, (("row", 0),), 2)
-        right_full = lax.all_gather(near_right, COL, axis=2, tiled=True)
+        right_full = jnp.concatenate(
+            lax.all_to_all(jnp.stack([near_right] * lax.axis_size(COL)), COL, 0, 0), axis=2
+        )
         square = jnp.where(kept, band_product(current, right_full), 0.0).astype(jnp.bfloat16)
         cubic = band_product(square, right_full)
         current = jnp.where(kept, 3.0 * square.astype(jnp.float32) - 2.0 * cubic, 0.0).astype(

time: 435 us -> 401 us (0.922)
  waiting for transfers between devices: 235 us -> 79.1 us
  blocking collectives: 24.1 us -> 148 us
    all_gather x2 -> x0, waiting for transfers between devices: 158 us -> none  [on_device(): right_full = lax.all_gather(near_right, COL, axis=2, tiled=True)]
    all_to_all x0 -> x2, blocking collectives: none -> 127 us  [on_device(): lax.all_to_all(jnp.stack([near_right] * lax.axis_size(COL)), COL, 0, 0)]
    slice x2 -> x12, local copies, waits for them, and re-layouts: 9.04 us -> 7.41 us  [band_product(): shifted = right_padded[offset_step:offset_step + blocks]]
  transfers between devices with their start and end apart: 12 -> 10, of which waited for: 11 -> 9; matrix products, arithmetic and copies ran while one was open for 0% -> 0% of each run, Pallas kernels for 0% -> 0%
where the time goes in v1:
time: 401 us; the launch traced here: 400 us
  blocking collectives  148 us (37%)
  waiting for transfers between devices  79.1 us (20%)
  local copies, waits for them, and re-layouts  49.2 us (12%)
  other arithmetic  48.1 us (12%)
  matrix products  30.3 us (8%)
  starting transfers between devices  26.2 us (7%)
  between operations  14.5 us (4%)
  loops' own time  5.51 us (1%)
    all_to_all x2, blocking collectives, on_device(): lax.all_to_all(jnp.stack([near_right] * lax.axis_size(COL)), COL, 0, 0)  127 us
    reduce_scatter x2, waiting for transfers between devices, sum_in_order(): pieces = lax.psum_scatter(pieces, axes[k], scatter_dimension=0, tiled=True)  50.5 us
    all_to_all x1, blocking collectives, sent_to_all(): lax.all_to_all(jnp.broadcast_to(value[None], (length, *value.shape)), axi...  20.9 us
    ppermute x3, waiting for transfers between devices, padded(): lax.ppermute(head, axis, [((i + 1) % count, i) for i in range(ends)])  20.8 us
    reduce_sum x2, other arithmetic, tile_terms(): jnp.sum(((2.0 * by_gradient * scaled)[None] * slopes)[:, :, None] * grads...  19.9 us
    ppermute x3, starting transfers between devices, padded(): lax.ppermute(tail, axis, [(i, (i + 1) % count) for i in range(ends)])  15.2 us
    dot_general x2, matrix products, tile_terms(): jnp.dot(values, window_block, preferred_element_type=jnp.float32)  14.7 us
    reduce_sum x2, other arithmetic, tile_terms(): jnp.sum(projected[None] * grads.astype(jnp.float32), axis=2)  13.6 us
  transfers between devices with their start and end apart: 10, of which 9 were waited for; matrix products, arithmetic and copies ran while one was open for 0% of the time, Pallas kernels for 0%

profile of v1, /device:TPU:7, one launch (start us, length us, event | category | flops | bytes accessed | tf_op | source)
XLA Modules:
  0.0 400.3 jit_solution(4066017568430894158)
XLA Ops:
  7.2 0.7 broadcast_compare_fusion
  8.0 1.1 copy_select_fusion
  9.1 4.0 %collective-permute-start = (bf16[2,5,32,256]{3,2,0,1:T(8,128)(2,1)S(1)}, bf16[2,5,32,256]{3,2,0,1:T(8,128)(2,1)S(1)}, u32[]{:S(2)}, u32[]{:S(2)}) collective-permute-start(bf16[2,5,32,256]{3,2,0,1:T(8,128)(2,1)S(1)} %get-tuple-element.391), channel_id=1, source_target_pairs={{0,8},{8,16},{16,24},{24,32},{32,40},{40,48},{48,56},{56,64},{64,7... | collective-permute-start | bytes 491528 | tf_op jit(solution)/shard_map/ppermute | solution.py:29
  13.1 1.9 collective-permute-start.1
  15.4 6.5 %collective-permute-done.1 = bf16[2,5,32,256]{3,2,0,1:T(8,128)(2,1)S(1)} collective-permute-done((bf16[2,5,32,256]{3,2,0,1:T(8,128)(2,1)S(1)}, bf16[2,5,32,256]{3,2,0,1:T(8,128)(2,1)S(1)}, u32[]{:S(2)}, u32[]{:S(2)}) %collective-permute-start.1) | collective-permute-done | bytes 163872 | tf_op jit(solution)/shard_map/ppermute | solution.py:31
  22.0 0.7 stack.121
  22.7 67.1 %all_to_all.15 = bf16[8,8,5,32,256]{4,3,2,1,0:T(8,128)(2,1)S(1)} all-to-all(bf16[8,8,5,32,256]{4,3,2,1,0:T(8,128)(2,1)S(1)} %stack.121), channel_id=1, replica_groups=mesh['row'=16,'col_0'=2,'col_1'=4] {'col_0','col_1'}, dimensions={0} | all-to-all | bytes 10485760 | tf_op jit(solution)/shard_map/all_to_all | solution.py:162
  89.8 2.2 fusion.161
  94.5 0.5 fusion.68
  96.8 0.5 fusion.65
  98.2 3.3 collective-permute-start.2
  101.6 1.9 collective-permute-start.3
  103.8 7.8 %collective-permute-done.3 = bf16[2,5,32,256]{3,2,0,1:T(8,128)(2,1)S(1)} collective-permute-done((bf16[2,5,32,256]{3,2,0,1:T(8,128)(2,1)S(1)}, bf16[2,5,32,256]{3,2,0,1:T(8,128)(2,1)S(1)}, u32[]{:S(2)}, u32[]{:S(2)}) %collective-permute-start.3) | collective-permute-done | bytes 163872 | tf_op jit(solution)/shard_map/ppermute | solution.py:31
  111.7 0.7 stack.122
  112.4 59.6 %all_to_all.16 = bf16[8,8,5,32,256]{4,3,2,1,0:T(8,128)(2,1)S(1)} all-to-all(bf16[8,8,5,32,256]{4,3,2,1,0:T(8,128)(2,1)S(1)} %stack.122), channel_id=1, replica_groups=mesh['row'=16,'col_0'=2,'col_1'=4] {'col_0','col_1'}, dimensions={0} | all-to-all | bytes 10485760 | tf_op jit(solution)/shard_map/all_to_all | solution.py:162
  172.0 2.2 fusion.160
  176.6 0.6 fusion.92
  177.1 0.5 fusion.98
  178.9 0.5 fusion.89
  179.4 0.5 fusion.95
  180.4 0.7 copy-done.4
  181.3 20.9 %all_to_all.17 = bf16[8,4,3,32,256]{4,3,2,1,0:T(8,128)(2,1)S(1)} all-to-all(bf16[8,4,3,32,256]{4,3,2,1,0:T(8,128)(2,1)S(1)} %broadcast_in_dim.83), channel_id=1, replica_groups=mesh['row'=16,'col_0'=2,'col_1'=4] {'col_0','col_1'}, dimensions={0} | all-to-all | bytes 3145728 | tf_op jit(solution)/shard_map/all_to_all | solution.py:46
  202.4 7.9 %collective-permute-start.4 = (bf16[1,3,256,256]{3,2,1,0:T(8,128)(2,1)S(1)}, bf16[1,3,256,256]{3,2,1,0:T(8,128)(2,1)S(1)}, u32[]{:S(2)}, u32[]{:S(2)}) collective-permute-start(bf16[1,3,256,256]{3,2,1,0:T(8,128)(2,1)S(1)} %bitcast.273), channel_id=1, source_target_pairs={{0,8},{8,16},{16,24},{24,32},{32,40},{40,48},{48,56},{56,64},{64,7... | collective-permute-start | bytes 1179656 | tf_op jit(solution)/shard_map/ppermute | solution.py:29
  210.3 2.1 collective-permute-start.5
  212.5 2.5 collective-permute-done.4
  215.0 6.5 %collective-permute-done.5 = bf16[1,3,256,256]{3,2,1,0:T(8,128)(2,1)S(1)} collective-permute-done((bf16[1,3,256,256]{3,2,1,0:T(8,128)(2,1)S(1)}, bf16[1,3,256,256]{3,2,1,0:T(8,128)(2,1)S(1)}, u32[]{:S(2)}, u32[]{:S(2)}) %collective-permute-start.5) | collective-permute-done | bytes 393248 | tf_op jit(solution)/shard_map/ppermute | solution.py:31
  221.5 1.7 pad_maximum_fusion
  223.2 2.6 broadcast_in_dim.81
  225.8 99.6 %while.18 = (s32[]{:T(128)}, f32[6,3,256,256]{3,2,1,0:T(8,128)}, f32[2,4096]{1,0:T(2,128)}, s32[2]{0:T(128)}, s32[]{:T(128)}, /*index=5*/bf16[2,4096,384]{2,1,0:...) while((s32[]{:T(128)}, f32[6,3,256,256]{3,2,1,0:T(8,128)}, ...), condition=%wide.region_5.6_spmd, body=%wide.region_0.5_spmd.sunk | while | flops 2456809472 | bytes 116916952 | solution.py:194
  225.8 1.3 dynamic_slice.135
  229.7 0.7 dynamic-slice_bitcast_fusion.5
  230.4 2.2 constant_dynamic-slice_fusion.2
  232.6 3.0 copy.354
  235.7 7.4 %multiply_reduce_fusion.4 = (f32[4096]{0:T(1024)S(1)}, f32[4096,384]{0,1:T(8,128)}) fusion(bf16[1,4096,384]{1,2,0:T(8,128)(2,1)} %copy.354, s32[]{:T(128)S(6)} %select_n.130, bf16[256,256]{1,0:T(8,128)(2,1)} %get-tuple-element.464, bf16[256,256]{1,0:T(8,128)(2,1)S(1)} %get-tuple-element.465, bf16[256,256]{1,0:T(8,128)(2,1)S(1)} %get-tuple-element.466, ...), kind=kOutput, calls=%fused_computation.6.clone.1 | convolution fusion | flops 1213853696 | bytes 13123588 | tf_op jit(solution)/shard_map/while/body/eval_jaxpr/dot_general | solution.py:84
  243.0 6.6 %copy.355 = f32[4096,384]{1,0:T(8,128)} copy(f32[4096,384]{0,1:T(8,128)} %get-tuple-element.468) | data formatting | bytes 12582912 | tf_op jit(solution)/shard_map/while/body/eval_jaxpr/dot_general | solution.py:84
  249.6 6.8 %fusion.177 = f32[3,4096]{1,0:T(4,128)S(1)} fusion(f32[4096,384]{1,0:T(8,128)} %copy.355, bf16[3,2,4096,384]{3,2,1,0:T(8,128)(2,1)} %get-tuple-element.523, s32[]{:T(128)} %get-tuple-element.497), kind=kLoop, calls=%fused_computation.2.clone.1 | loop fusion | flops 14143488 | bytes 15777796 | tf_op jit(solution)/shard_map/while/body/eval_jaxpr/reduce_sum | solution.py:86
  256.9 9.9 %fusion.178 = f32[4096,384]{1,0:T(8,128)S(1)} fusion(f32[3,4096]{1,0:T(4,128)S(1)} %broadcast_multiply_fusion.5, bf16[3,2,4096,384]{3,2,1,0:T(8,128)(2,1)} %get-tuple-element.523, s32[]{:T(128)} %get-tuple-element.497), kind=kLoop, calls=%fused_computation.3.clone.1 | loop fusion | flops 12582912 | bytes 15777796 | tf_op jit(solution)/shard_map/while/body/eval_jaxpr/reduce_sum | solution.py:91
  266.9 3.2 fusion.180
  270.1 1.4 copy.356
  272.0 2.9 fusion.182
  275.0 0.6 copy-done.10
  275.7 1.3 dynamic_slice.135
  279.6 0.7 dynamic-slice_bitcast_fusion.5
  280.3 2.2 constant_dynamic-slice_fusion.2
  282.5 3.0 copy.354
  285.5 7.3 %multiply_reduce_fusion.4 = (f32[4096]{0:T(1024)S(1)}, f32[4096,384]{0,1:T(8,128)}) fusion(bf16[1,4096,384]{1,2,0:T(8,128)(2,1)} %copy.354, s32[]{:T(128)S(6)} %select_n.130, bf16[256,256]{1,0:T(8,128)(2,1)} %get-tuple-element.464, bf16[256,256]{1,0:T(8,128)(2,1)S(1)} %get-tuple-element.465, bf16[256,256]{1,0:T(8,128)(2,1)S(1)} %get-tuple-element.466, ...), kind=kOutput, calls=%fused_computation.6.clone.1 | convolution fusion | flops 1213853696 | bytes 13123588 | tf_op jit(solution)/shard_map/while/body/eval_jaxpr/dot_general | solution.py:84
  292.8 6.6 %copy.355 = f32[4096,384]{1,0:T(8,128)} copy(f32[4096,384]{0,1:T(8,128)} %get-tuple-element.468) | data formatting | bytes 12582912 | tf_op jit(solution)/shard_map/while/body/eval_jaxpr/dot_general | solution.py:84
  299.4 6.8 %fusion.177 = f32[3,4096]{1,0:T(4,128)S(1)} fusion(f32[4096,384]{1,0:T(8,128)} %copy.355, bf16[3,2,4096,384]{3,2,1,0:T(8,128)(2,1)} %get-tuple-element.523, s32[]{:T(128)} %get-tuple-element.497), kind=kLoop, calls=%fused_computation.2.clone.1 | loop fusion | flops 14143488 | bytes 15777796 | tf_op jit(solution)/shard_map/while/body/eval_jaxpr/reduce_sum | solution.py:86
  306.7 9.9 %fusion.178 = f32[4096,384]{1,0:T(8,128)S(1)} fusion(f32[3,4096]{1,0:T(4,128)S(1)} %broadcast_multiply_fusion.5, bf16[3,2,4096,384]{3,2,1,0:T(8,128)(2,1)} %get-tuple-element.523, s32[]{:T(128)} %get-tuple-element.497), kind=kLoop, calls=%fused_computation.3.clone.1 | loop fusion | flops 12582912 | bytes 15777796 | tf_op jit(solution)/shard_map/while/body/eval_jaxpr/reduce_sum | solution.py:91
  316.7 3.2 fusion.180
  319.9 1.4 copy.356
  321.7 2.9 fusion.182
  324.8 0.6 copy-done.10
  325.4 2.6 convert_element_type.116
  328.1 1.7 copy.203
  329.9 29.0 %reduce-scatter.3.cloned.1.call-done = bf16[2,6,3,32,256]{4,3,2,1,0:T(8,128)(2,1)} async-done(((bf16[8,6,3,32,256]{4,3,2,1,0:T(8,128)(2,1)}), bf16[2,6,3,32,256]{4,3,2,1,0:T(8,128)(2,1)}) %reduce-scatter.3.cloned.1.call-update) | async-done | bytes 589840 | tf_op jit(solution)/shard_map/reduce_scatter | solution.py:60
  358.9 21.5 %reduce-scatter.5.cloned.1.call-done = bf16[1,6,3,32,256]{4,3,2,1,0:T(8,128)(2,1)} async-done(((bf16[2,6,3,32,256]{4,3,2,1,0:T(8,128)(2,1)}), bf16[1,6,3,32,256]{4,3,2,1,0:T(8,128)(2,1)}) %reduce-scatter.5.cloned.1.call-update) | async-done | bytes 294928 | tf_op jit(solution)/shard_map/reduce_scatter | solution.py:60
  380.4 0.8 slice_bitcast_fusion.48
  381.2 3.0 collective-permute-start.6
  384.2 0.7 copy.207
  385.0 1.9 collective-permute-start.7
  386.9 1.0 convert_element_type.117
  388.0 4.5 %collective-permute-done.7 = bf16[3,32,256]{2,1,0:T(8,128)(2,1)S(1)} collective-permute-done((bf16[3,32,256]{2,1,0:T(8,128)(2,1)S(1)}, bf16[3,32,256]{2,1,0:T(8,128)(2,1)S(1)}, u32[]{:S(2)}, u32[]{:S(2)}) %collective-permute-start.7) | collective-permute-done | bytes 49184 | tf_op jit(solution)/shard_map/ppermute | solution.py:18
  392.6 0.9 copy.208
  (100 shorter events, 12.8 us)
Async XLA Ops:
  7.2 351.7 %reduce-scatter.3.cloned.1.call-start = ((), (), s32[]{:S(2)}) async-start(), calls=%async_computation.5 | async-start | bytes 2949120 | tf_op jit(solution)/shard_map/reduce_scatter | solution.py:60
  8.0 171.9 %copy-start.7 = (pred[4,5]{0,1:T(8,128)(4,1)}, pred[4,5]{0,1:T(8,128)(4,1)S(1)}, u32[]{:S(2)}) copy-start(pred[4,5]{0,1:T(8,128)(4,1)S(1)} %copy.164) | copy-start | bytes 64
  9.1 6.3 %collective-permute-start = (bf16[2,5,32,256]{3,2,0,1:T(8,128)(2,1)S(1)}, bf16[2,5,32,256]{3,2,0,1:T(8,128)(2,1)S(1)}, u32[]{:S(2)}, u32[]{:S(2)}) collective-permute-start(bf16[2,5,32,256]{3,2,0,1:T(8,128)(2,1)S(1)} %get-tuple-element.391), channel_id=1, source_target_pairs={{0,8},{8,16},{16,24},{24,32},{32,40},{40,48},{48,56},{56,64},{64,7... | collective-permute-start | bytes 491528 | tf_op jit(solution)/shard_map/ppermute | solution.py:29
  13.1 8.7 %collective-permute-start.1 = (bf16[2,5,32,256]{3,2,0,1:T(8,128)(2,1)S(1)}, bf16[2,5,32,256]{3,2,0,1:T(8,128)(2,1)S(1)}, u32[]{:S(2)}, u32[]{:S(2)}) collective-permute-start(bf16[2,5,32,256]{3,2,0,1:T(8,128)(2,1)S(1)} %get-tuple-element.392), channel_id=1, source_target_pairs={{8,0},{16,8},{24,16},{32,24},{40,32},{48,40},{56,48},{64,56},{72,6... | collective-permute-start | bytes 491528 | tf_op jit(solution)/shard_map/ppermute | solution.py:31
  98.2 5.6 %collective-permute-start.2 = (bf16[2,5,32,256]{3,2,0,1:T(8,128)(2,1)S(1)}, bf16[2,5,32,256]{3,2,0,1:T(8,128)(2,1)S(1)}, u32[]{:S(2)}, u32[]{:S(2)}) collective-permute-start(bf16[2,5,32,256]{3,2,0,1:T(8,128)(2,1)S(1)} %get-tuple-element.389), channel_id=1, source_target_pairs={{0,8},{8,16},{16,24},{24,32},{32,40},{40,48},{48,56},{56,64},{64,7... | collective-permute-start | bytes 491528 | tf_op jit(solution)/shard_map/ppermute | solution.py:29
  101.6 10.0 %collective-permute-start.3 = (bf16[2,5,32,256]{3,2,0,1:T(8,128)(2,1)S(1)}, bf16[2,5,32,256]{3,2,0,1:T(8,128)(2,1)S(1)}, u32[]{:S(2)}, u32[]{:S(2)}) collective-permute-start(bf16[2,5,32,256]{3,2,0,1:T(8,128)(2,1)S(1)} %get-tuple-element.390), channel_id=1, source_target_pairs={{8,0},{16,8},{24,16},{32,24},{40,32},{48,40},{56,48},{64,56},{72,6... | collective-permute-start | bytes 491528 | tf_op jit(solution)/shard_map/ppermute | solution.py:31
  180.4 0.7 copy-start.4
  202.3 19.2 %copy-start.3 = (bf16[8,4,3,32,256]{4,3,0,2,1:T(8,128)(2,1)}, bf16[8,4,3,32,256]{4,3,0,2,1:T(8,128)(2,1)S(1)}, u32[]{:S(2)}) copy-start(bf16[8,4,3,32,256]{4,3,0,2,1:T(8,128)(2,1)S(1)} %copy.350) | copy-start | bytes 4718596
  202.4 12.6 %collective-permute-start.4 = (bf16[1,3,256,256]{3,2,1,0:T(8,128)(2,1)S(1)}, bf16[1,3,256,256]{3,2,1,0:T(8,128)(2,1)S(1)}, u32[]{:S(2)}, u32[]{:S(2)}) collective-permute-start(bf16[1,3,256,256]{3,2,1,0:T(8,128)(2,1)S(1)} %bitcast.273), channel_id=1, source_target_pairs={{0,8},{8,16},{16,24},{24,32},{32,40},{40,48},{48,56},{56,64},{64,7... | collective-permute-start | bytes 1179656 | tf_op jit(solution)/shard_map/ppermute | solution.py:29
  210.3 11.2 %collective-permute-start.5 = (bf16[1,3,256,256]{3,2,1,0:T(8,128)(2,1)S(1)}, bf16[1,3,256,256]{3,2,1,0:T(8,128)(2,1)S(1)}, u32[]{:S(2)}, u32[]{:S(2)}) collective-permute-start(bf16[1,3,256,256]{3,2,1,0:T(8,128)(2,1)S(1)} %bitcast.272), channel_id=1, source_target_pairs={{8,0},{16,8},{24,16},{32,24},{40,32},{48,40},{56,48},{64,56},{72,6... | collective-permute-start | bytes 1179656 | tf_op jit(solution)/shard_map/ppermute | solution.py:31
  225.8 4.6 %copy-start.1 = (bf16[6,3,256,256]{3,2,1,0:T(8,128)(2,1)}, bf16[6,3,256,256]{3,2,1,0:T(8,128)(2,1)S(1)}, u32[]{:S(2)}) copy-start(bf16[6,3,256,256]{3,2,1,0:T(8,128)(2,1)S(1)} %get-tuple-element.522) | copy-start | bytes 7077892 | tf_op jit(solution)/shard_map/while
  249.6 6.9 %copy-start.6 = (f32[2,4096]{1,0:T(2,128)S(1)}, f32[2,4096]{1,0:T(2,128)}, u32[]{:S(2)}) copy-start(f32[2,4096]{1,0:T(2,128)} %get-tuple-element.524) | copy-start | bytes 98308 | tf_op jit(solution)/shard_map/while
  270.1 1.5 copy-start
  271.9 3.0 copy-start.9
  272.0 3.7 copy-start.2
  275.0 0.6 copy-start.10
  275.7 4.6 %copy-start.1 = (bf16[6,3,256,256]{3,2,1,0:T(8,128)(2,1)}, bf16[6,3,256,256]{3,2,1,0:T(8,128)(2,1)S(1)}, u32[]{:S(2)}) copy-start(bf16[6,3,256,256]{3,2,1,0:T(8,128)(2,1)S(1)} %get-tuple-element.522) | copy-start | bytes 7077892 | tf_op jit(solution)/shard_map/while
  299.4 6.9 %copy-start.6 = (f32[2,4096]{1,0:T(2,128)S(1)}, f32[2,4096]{1,0:T(2,128)}, u32[]{:S(2)}) copy-start(f32[2,4096]{1,0:T(2,128)} %get-tuple-element.524) | copy-start | bytes 98308 | tf_op jit(solution)/shard_map/while
  319.9 1.5 copy-start
  321.7 2.9 copy-start.9
  321.7 3.7 copy-start.2
  324.8 0.6 copy-start.10
  329.8 54.4 %copy-start.5 = (bf16[4,5,32,256]{3,2,0,1:T(8,128)(2,1)S(1)}, bf16[4,5,32,256]{3,2,0,1:T(8,128)(2,1)}, u32[]{:S(2)}) copy-start(bf16[4,5,32,256]{3,2,0,1:T(8,128)(2,1)} %copy-done.4) | copy-start | bytes 983044
  329.8 62.7 %copy-start.8 = (pred[4,5]{0,1:T(8,128)(4,1)S(1)}, pred[4,5]{0,1:T(8,128)(4,1)}, u32[]{:S(2)}) copy-start(pred[4,5]{0,1:T(8,128)(4,1)} %copy-done.7) | copy-start | bytes 64
  329.8 50.6 %reduce-scatter.5.cloned.1.call-start = ((), (), s32[]{:S(2)}) async-start(), calls=%async_computation.6 | async-start | bytes 884736 | tf_op jit(solution)/shard_map/reduce_scatter | solution.py:60
  381.2 6.7 %collective-permute-start.6 = (bf16[3,32,256]{2,1,0:T(8,128)(2,1)S(1)}, bf16[3,32,256]{2,1,0:T(8,128)(2,1)S(1)}, u32[]{:S(2)}, u32[]{:S(2)}) collective-permute-start(bf16[3,32,256]{2,1,0:T(8,128)(2,1)S(1)} %get-tuple-element.393), channel_id=1, source_target_pairs={{0,8},{8,16},{16,24},{24,32},{32,40},{40,48},{48,56},{56,64},{64,7... | collective-permute-start | bytes 147464 | tf_op jit(solution)/shard_map/ppermute | solution.py:18
  385.0 7.5 %collective-permute-start.7 = (bf16[3,32,256]{2,1,0:T(8,128)(2,1)S(1)}, bf16[3,32,256]{2,1,0:T(8,128)(2,1)S(1)}, u32[]{:S(2)}, u32[]{:S(2)}) collective-permute-start(bf16[3,32,256]{2,1,0:T(8,128)(2,1)S(1)} %get-tuple-element.394), channel_id=1, source_target_pairs={{8,0},{16,8},{24,16},{32,24},{40,32},{48,40},{56,48},{64,56},{72,6... | collective-permute-start | bytes 147464 | tf_op jit(solution)/shard_map/ppermute | solution.py:18
Sparse Core Ops, SparseCore 0:
  330.0 28.8 reduce-scatter.2
  361.2 19.1 reduce-scatter.4
